TPU v7x, 128 devices: a whole 4x4x4 slice. The times are simulated.
128 devices in a mesh: dp: 32 (over y, z, core), mp: 4 (over x).
Axes of the slice: x: 4, y: 4, z: 4, core: 2. Of those that a mesh axis runs over, the one named last changes fastest.
Arguments:
- table: float32 [262144, 512], P('dp', 'mp'), may hold values from -6 to 6
- first_moment: float32 [262144, 512], P('dp', 'mp'), may hold values from -1.8 to 1.8
- second_moment: float32 [262144, 512], P('dp', 'mp'), may hold values from 0.01 to 1
- grads: bfloat16 [65536, 512], P('dp', 'mp'), may hold values from -108 to 108
- ids: int32 [65536], P('dp'), may hold values from 0 to 262143, as said below
Outputs:
- new_table: float32 [262144, 512], P('dp', 'mp')
- new_first: float32 [262144, 512], P('dp', 'mp')
- new_second: float32 [262144, 512], P('dp', 'mp')
Inputs may be any that keep to these rules, and one draw needn't show every extreme that they name: `ids`: the positions of one device name at most 256 positions' worth of rows of any one owner (rows k * 8192 to (k + 1) * 8192 - 1) and at most 64 distinct rows of one owner; in every draw one owner reaches both bounds on every device.
All inputs are finite; a program needn't handle non-finite values.
Results may differ from a plain program's by a relative error of at most 0.0003.
Values may be sent and summed in bfloat16 or wider, within the bound.
A program may use at most 64 MiB of HBM per device.

v0:
```python
import jax
import jax.numpy as jnp
from jax import lax
from jax.sharding import Mesh
from jax.sharding import PartitionSpec as P

DP = ("dp_0", "dp_1", "dp_2")
DP_MP = ("dp_0", "dp_1", "dp_2", "mp")
beta_first = 0.9
beta_second = 0.999
learn_rate = 0.01
decay_rate = 0.1
adam_eps = 1e-08
first_fix = 0.9999734386
second_fix = 0.0952078529


def by_axis(shard, axes):
    for axis in axes:
        shard = lax.psum(shard, axis)
    return shard


def block_size():
    return 512


def block_starts(count, step):
    return jnp.arange(0, count, step, dtype=jnp.int32)


def pack_slots(dest, local_row, values, slots, rows_dev):
    step = block_size()

    def pack_one_block(start):
        target = start + jnp.arange(step, dtype=jnp.int32)
        match = dest[None, :] == target[:, None]
        summed = jnp.dot(match.astype(jnp.bfloat16), values, preferred_element_type=jnp.float32)
        marks = jnp.min(jnp.where(match, local_row[None, :], rows_dev), axis=1)
        return (summed, marks)

    summed, marks = lax.map(pack_one_block, block_starts(slots, step))
    return (summed.reshape(slots, values.shape[1]), marks.reshape(slots))


def gather_rows(got_row, got, rows_dev):
    step = block_size()

    def gather_one_block(start):
        target = start + jnp.arange(step, dtype=jnp.int32)
        match = got_row[None, :] == target[:, None]
        return jnp.dot(
            match.astype(jnp.float32),
            got,
            precision=lax.Precision.HIGHEST,
            preferred_element_type=jnp.float32,
        )

    return lax.map(gather_one_block, block_starts(rows_dev, step)).reshape(rows_dev, got.shape[1])


def body(table, first_moment, second_moment, grads, ids):
    peers = lax.axis_size(DP)
    rows_dev = table.shape[0]
    width = table.shape[1]
    tok_dev = grads.shape[0]
    room = tok_dev // peers
    owner = ids // rows_dev
    local_row = ids - owner * rows_dev
    place = jnp.arange(tok_dev, dtype=jnp.int32)
    step = block_size()

    def first_block(start):
        here = start + jnp.arange(step, dtype=jnp.int32)
        mine = lax.dynamic_slice_in_dim(ids, start, step)
        earlier = jnp.logical_and(ids[None, :] == mine[:, None], place[None, :] < here[:, None])
        return jnp.logical_not(jnp.any(earlier, axis=1))

    leading = lax.map(first_block, block_starts(tok_dev, step)).reshape(tok_dev)

    def rank_block(start):
        mine = lax.dynamic_slice_in_dim(ids, start, step)
        mine_owner = lax.dynamic_slice_in_dim(owner, start, step)
        below = (
            leading[None, :]
            & (owner[None, :] == mine_owner[:, None])
            & (ids[None, :] < mine[:, None])
        )
        return jnp.sum(below.astype(jnp.int32), axis=1)

    rank = lax.map(rank_block, block_starts(tok_dev, step)).reshape(tok_dev)
    dest = owner * room + rank
    slots = peers * room
    sums, marker = pack_slots(dest, local_row, grads, slots, rows_dev)
    row_marks = marker.astype(jnp.float32).reshape(peers, room)
    got, got_rows = (
        lax.all_to_all(
            sums.reshape(peers, room, width), DP, split_axis=0, concat_axis=0, tiled=True
        ),
        lax.all_to_all(row_marks, DP, split_axis=0, concat_axis=0, tiled=True),
    )
    got_index = got_rows.reshape(slots).astype(jnp.int32)
    grad_rows = gather_rows(got_index, got.reshape(slots, width), rows_dev)
    local_sum = jnp.sum(grad_rows * grad_rows)
    total = by_axis(local_sum, DP_MP)
    limit = jnp.sqrt(jnp.float32(tok_dev * peers * width * lax.axis_size("mp")))
    scale = limit / jnp.maximum(jnp.sqrt(total), limit)
    clipped = scale * grad_rows
    new_first = beta_first * first_moment + (1.0 - beta_first) * clipped
    new_second = beta_second * second_moment + (1.0 - beta_second) * clipped * clipped
    first_hat = new_first / first_fix
    second_hat = new_second / second_fix
    new_table = table - learn_rate * (
        first_hat / (jnp.sqrt(second_hat) + adam_eps) + decay_rate * table
    )
    return (new_table, new_first, new_second)


def solution(mesh):
    split = Mesh(mesh.devices.reshape(4, 4, 2, mesh.shape["mp"]), ("dp_0", "dp_1", "dp_2", "mp"))
    placed = (P(DP, "mp"), P(DP, "mp"), P(DP, "mp"), P(DP, "mp"), P(DP))
    return jax.shard_map(
        body,
        mesh=split,
        in_specs=placed,
        out_specs=(P(DP, "mp"), P(DP, "mp"), P(DP, "mp")),
        check_vma=False,
    )
```

profile of v0, /device:TPU:0, one launch (start us, length us, event | category | flops | bytes accessed | tf_op | source)
XLA Modules:
  0.0 212.3 jit_solution(10993238454056998572)
XLA Ops:
  0.7 0.7 add_select_fusion
  1.4 22.3 %while.46 = (s32[]{:T(128)}, pred[4,512]{1,0:T(4,128)(4,1)S(1)}, s32[2048]{0:T(1024)}, s32[4]{0:T(128)S(1)}, s32[]{:T(128)}, /*index=5*/s32[]{:T(128)}, s32[]{:T(128)}) while((s32[]{:T(128)}, pred[4,512]{1,0:T(4,128)(4,1)S(1)}, s32[2048]{0:T(1024)}, s32[4]{0:T(128)S(1)}, s32[]{:T(128)}, /*index=5*/s32[]{:T(128)}, s32[]{:T(128)}) %tuple.67), condition=%wide.region_2.3_spmd.clone, body=%wide.region_0.2_spmd.clone.sunk | while | flops 4194821 | bytes 22159 | solution.py:79
  4.2 0.8 dynamic_slice.38
  5.0 1.9 fusion.48
  9.8 0.8 dynamic_slice.38
  10.6 1.9 fusion.48
  15.4 0.8 dynamic_slice.38
  16.1 1.9 fusion.48
  20.9 0.8 dynamic_slice.38
  21.7 1.9 fusion.48
  23.7 20.1 %while.43 = (s32[]{:T(128)}, s32[4,512]{1,0:T(4,128)S(1)}, pred[4,512]{1,0:T(4,128)(4,1)S(1)}, s32[2048]{0:T(1024)S(1)}, s32[4]{0:T(128)S(1)}, /*index=5*/s32[2048]{0:T(1024)}, s32[]{:T(128)}, s32[]{:T(128)}, s32[]{:T(128)}) while((s32[]{:T(128)}, s32[4,512]{1,0:T(4,128)S(1)}, pred[4,512]{1,0:T(4,128)(4,1)S(1)}, s32[2048]{0:T(1024)S(1)}, ...), condition=%wide.region_5.6_spmd, body=%wide.region_3.5_spmd.sunk | while | flops 6290949 | bytes 41119 | solution.py:91
  26.1 0.8 dynamic_slice.33
  26.8 1.8 convert_reduce_fusion.3
  31.1 0.8 dynamic_slice.33
  31.9 1.8 convert_reduce_fusion.3
  36.1 0.8 dynamic_slice.33
  36.9 1.8 convert_reduce_fusion.3
  41.1 0.8 dynamic_slice.33
  41.9 1.8 convert_reduce_fusion.3
  43.8 0.7 multiply_subtract_fusion.1
  44.5 18.4 %while.44 = (s32[]{:T(128)}, f32[4,512,128]{2,1,0:T(8,128)}, s32[4,512]{1,0:T(4,128)S(1)}, s32[2048]{0:T(1024)S(1)}, s32[4]{0:T(128)S(1)}, /*index=5*/bf16[2048,...) while((s32[]{:T(128)}, f32[4,512,128]{2,1,0:T(8,128)}, s32[4,512]{1,0:T(4,128)S(1)}, ...), condition=%wide.region_8.9_spmd, body=%wide.region_6.8_spmd.sunk | while | flops 272629760 | bytes 823421 | solution.py:42
  44.5 0.7 dynamic_slice.35
  45.2 0.7 iota_add_fusion.6
  45.9 0.7 fusion.44
  46.6 2.5 %fusion.43 = f32[4,512,128]{2,1,0:T(8,128)} fusion(f32[4,512,128]{2,1,0:T(8,128)} %get-tuple-element.385, s32[]{:T(128)S(6)} %copy.32, bf16[2048,128]{1,0:T(8,128)(2,1)} %get-tuple-element.398, s32[2048]{0:T(1024)S(1)} %get-tuple-element.396, s32[512]{0:T(512)S(1)} %iota_add_fusion.6), kind=kOutput, calls=%fused_computation.9.clone.1 | convolution fusion | flops 269484032 | bytes 796676 | tf_op jit(solution)/shard_map/while/body/eval_jaxpr/dot_general | solution.py:38
  49.1 0.7 dynamic_slice.35
  49.8 0.7 iota_add_fusion.6
  50.5 0.7 fusion.44
  51.2 2.5 %fusion.43 = f32[4,512,128]{2,1,0:T(8,128)} fusion(f32[4,512,128]{2,1,0:T(8,128)} %get-tuple-element.385, s32[]{:T(128)S(6)} %copy.32, bf16[2048,128]{1,0:T(8,128)(2,1)} %get-tuple-element.398, s32[2048]{0:T(1024)S(1)} %get-tuple-element.396, s32[512]{0:T(512)S(1)} %iota_add_fusion.6), kind=kOutput, calls=%fused_computation.9.clone.1 | convolution fusion | flops 269484032 | bytes 796676 | tf_op jit(solution)/shard_map/while/body/eval_jaxpr/dot_general | solution.py:38
  54.4 0.7 iota_add_fusion.6
  55.1 0.7 fusion.44
  55.8 2.5 %fusion.43 = f32[4,512,128]{2,1,0:T(8,128)} fusion(f32[4,512,128]{2,1,0:T(8,128)} %get-tuple-element.385, s32[]{:T(128)S(6)} %copy.32, bf16[2048,128]{1,0:T(8,128)(2,1)} %get-tuple-element.398, s32[2048]{0:T(1024)S(1)} %get-tuple-element.396, s32[512]{0:T(512)S(1)} %iota_add_fusion.6), kind=kOutput, calls=%fused_computation.9.clone.1 | convolution fusion | flops 269484032 | bytes 796676 | tf_op jit(solution)/shard_map/while/body/eval_jaxpr/dot_general | solution.py:38
  59.0 0.7 iota_add_fusion.6
  59.7 0.7 fusion.44
  60.4 2.5 %fusion.43 = f32[4,512,128]{2,1,0:T(8,128)} fusion(f32[4,512,128]{2,1,0:T(8,128)} %get-tuple-element.385, s32[]{:T(128)S(6)} %copy.32, bf16[2048,128]{1,0:T(8,128)(2,1)} %get-tuple-element.398, s32[2048]{0:T(1024)S(1)} %get-tuple-element.396, s32[512]{0:T(512)S(1)} %iota_add_fusion.6), kind=kOutput, calls=%fused_computation.9.clone.1 | convolution fusion | flops 269484032 | bytes 796676 | tf_op jit(solution)/shard_map/while/body/eval_jaxpr/dot_general | solution.py:38
  63.0 15.6 %all_to_all.11 = f32[32,1,64]{2,1,0:T(1,128)S(1)} all-to-all(f32[32,1,64]{2,1,0:T(1,128)S(1)} %convert_element_type.26), channel_id=1, replica_groups=mesh['dp_0'=4,'dp_1'=4,'dp_2'=2,'mp'=4] {'dp_0','dp_1','dp_2'}, dimensions={0} | all-to-all | bytes 16384 | tf_op jit(solution)/shard_map/all_to_all | solution.py:100
  78.7 3.9 %all-to-all-start.1 = ((f32[32,64,128]{2,1,0:T(8,128)}), f32[32,64,128]{2,1,0:T(8,128)S(1)}, u32[]{:S(2)}, u32[]{:S(2)}) async-start(f32[32,64,128]{2,1,0:T(8,128)} %bitcast.7), calls=%async_computation.1 | async-start | bytes 2097152 | tf_op jit(solution)/shard_map/all_to_all | solution.py:97
  82.8 16.6 %all-to-all-done.1 = f32[32,64,128]{2,1,0:T(8,128)S(1)} async-done(((f32[32,64,128]{2,1,0:T(8,128)}), f32[32,64,128]{2,1,0:T(8,128)S(1)}, u32[]{:S(2)}, u32[]{:S(2)}) %all-to-all-start.1) | async-done | bytes 1048608 | tf_op jit(solution)/shard_map/all_to_all | solution.py:97
  99.4 62.8 %while.45 = (s32[]{:T(128)}, f32[16,512,128]{2,1,0:T(8,128)}, s32[2048]{0:T(1024)S(1)}, s32[16]{0:T(128)S(1)}, f32[2048,128]{1,0:T(8,128)S(1)}, /*index=5*/s32[]{:T(128)}) while((s32[]{:T(128)}, f32[16,512,128]{2,1,0:T(8,128)}, s32[2048]{0:T(1024)S(1)}, s32[16]{0:T(128)S(1)}, f32[2048,128]{1,0:T(8,128)S(1)}, /*index=5*/s32[]{:T(128)}) %tuple.79), condition=%wide.region_10.11_spmd, body=%wide.region_9.10_spmd.sunk | while | flops 1611661824 | bytes 1323105 | solution.py:59
  100.6 2.7 %fusion.47 = f32[16,512,128]{2,1,0:T(8,128)} fusion(f32[16,512,128]{2,1,0:T(8,128)} %get-tuple-element.409, s32[]{:T(128)S(6)} %copy.40, f32[2048,128]{1,0:T(8,128)S(1)} %get-tuple-element.418, s32[2048]{0:T(1024)S(1)} %get-tuple-element.416, s32[512]{0:T(512)S(1)} %iota_add_fusion.7), kind=kOutput, calls=%fused_computation.16.clone.1 | convolution fusion | flops 1611661312 | bytes 1320964 | tf_op jit(solution)/shard_map/while/body/eval_jaxpr/dot_general | solution.py:52
  104.5 2.7 %fusion.47 = f32[16,512,128]{2,1,0:T(8,128)} fusion(f32[16,512,128]{2,1,0:T(8,128)} %get-tuple-element.409, s32[]{:T(128)S(6)} %copy.40, f32[2048,128]{1,0:T(8,128)S(1)} %get-tuple-element.418, s32[2048]{0:T(1024)S(1)} %get-tuple-element.416, s32[512]{0:T(512)S(1)} %iota_add_fusion.7), kind=kOutput, calls=%fused_computation.16.clone.1 | convolution fusion | flops 1611661312 | bytes 1320964 | tf_op jit(solution)/shard_map/while/body/eval_jaxpr/dot_general | solution.py:52
  108.5 2.7 %fusion.47 = f32[16,512,128]{2,1,0:T(8,128)} fusion(f32[16,512,128]{2,1,0:T(8,128)} %get-tuple-element.409, s32[]{:T(128)S(6)} %copy.40, f32[2048,128]{1,0:T(8,128)S(1)} %get-tuple-element.418, s32[2048]{0:T(1024)S(1)} %get-tuple-element.416, s32[512]{0:T(512)S(1)} %iota_add_fusion.7), kind=kOutput, calls=%fused_computation.16.clone.1 | convolution fusion | flops 1611661312 | bytes 1320964 | tf_op jit(solution)/shard_map/while/body/eval_jaxpr/dot_general | solution.py:52
  112.4 2.7 %fusion.47 = f32[16,512,128]{2,1,0:T(8,128)} fusion(f32[16,512,128]{2,1,0:T(8,128)} %get-tuple-element.409, s32[]{:T(128)S(6)} %copy.40, f32[2048,128]{1,0:T(8,128)S(1)} %get-tuple-element.418, s32[2048]{0:T(1024)S(1)} %get-tuple-element.416, s32[512]{0:T(512)S(1)} %iota_add_fusion.7), kind=kOutput, calls=%fused_computation.16.clone.1 | convolution fusion | flops 1611661312 | bytes 1320964 | tf_op jit(solution)/shard_map/while/body/eval_jaxpr/dot_general | solution.py:52
  116.3 2.7 %fusion.47 = f32[16,512,128]{2,1,0:T(8,128)} fusion(f32[16,512,128]{2,1,0:T(8,128)} %get-tuple-element.409, s32[]{:T(128)S(6)} %copy.40, f32[2048,128]{1,0:T(8,128)S(1)} %get-tuple-element.418, s32[2048]{0:T(1024)S(1)} %get-tuple-element.416, s32[512]{0:T(512)S(1)} %iota_add_fusion.7), kind=kOutput, calls=%fused_computation.16.clone.1 | convolution fusion | flops 1611661312 | bytes 1320964 | tf_op jit(solution)/shard_map/while/body/eval_jaxpr/dot_general | solution.py:52
  120.2 2.7 %fusion.47 = f32[16,512,128]{2,1,0:T(8,128)} fusion(f32[16,512,128]{2,1,0:T(8,128)} %get-tuple-element.409, s32[]{:T(128)S(6)} %copy.40, f32[2048,128]{1,0:T(8,128)S(1)} %get-tuple-element.418, s32[2048]{0:T(1024)S(1)} %get-tuple-element.416, s32[512]{0:T(512)S(1)} %iota_add_fusion.7), kind=kOutput, calls=%fused_computation.16.clone.1 | convolution fusion | flops 1611661312 | bytes 1320964 | tf_op jit(solution)/shard_map/while/body/eval_jaxpr/dot_general | solution.py:52
  124.2 2.7 %fusion.47 = f32[16,512,128]{2,1,0:T(8,128)} fusion(f32[16,512,128]{2,1,0:T(8,128)} %get-tuple-element.409, s32[]{:T(128)S(6)} %copy.40, f32[2048,128]{1,0:T(8,128)S(1)} %get-tuple-element.418, s32[2048]{0:T(1024)S(1)} %get-tuple-element.416, s32[512]{0:T(512)S(1)} %iota_add_fusion.7), kind=kOutput, calls=%fused_computation.16.clone.1 | convolution fusion | flops 1611661312 | bytes 1320964 | tf_op jit(solution)/shard_map/while/body/eval_jaxpr/dot_general | solution.py:52
  128.1 2.7 %fusion.47 = f32[16,512,128]{2,1,0:T(8,128)} fusion(f32[16,512,128]{2,1,0:T(8,128)} %get-tuple-element.409, s32[]{:T(128)S(6)} %copy.40, f32[2048,128]{1,0:T(8,128)S(1)} %get-tuple-element.418, s32[2048]{0:T(1024)S(1)} %get-tuple-element.416, s32[512]{0:T(512)S(1)} %iota_add_fusion.7), kind=kOutput, calls=%fused_computation.16.clone.1 | convolution fusion | flops 1611661312 | bytes 1320964 | tf_op jit(solution)/shard_map/while/body/eval_jaxpr/dot_general | solution.py:52
  132.0 2.7 %fusion.47 = f32[16,512,128]{2,1,0:T(8,128)} fusion(f32[16,512,128]{2,1,0:T(8,128)} %get-tuple-element.409, s32[]{:T(128)S(6)} %copy.40, f32[2048,128]{1,0:T(8,128)S(1)} %get-tuple-element.418, s32[2048]{0:T(1024)S(1)} %get-tuple-element.416, s32[512]{0:T(512)S(1)} %iota_add_fusion.7), kind=kOutput, calls=%fused_computation.16.clone.1 | convolution fusion | flops 1611661312 | bytes 1320964 | tf_op jit(solution)/shard_map/while/body/eval_jaxpr/dot_general | solution.py:52
  135.9 2.7 %fusion.47 = f32[16,512,128]{2,1,0:T(8,128)} fusion(f32[16,512,128]{2,1,0:T(8,128)} %get-tuple-element.409, s32[]{:T(128)S(6)} %copy.40, f32[2048,128]{1,0:T(8,128)S(1)} %get-tuple-element.418, s32[2048]{0:T(1024)S(1)} %get-tuple-element.416, s32[512]{0:T(512)S(1)} %iota_add_fusion.7), kind=kOutput, calls=%fused_computation.16.clone.1 | convolution fusion | flops 1611661312 | bytes 1320964 | tf_op jit(solution)/shard_map/while/body/eval_jaxpr/dot_general | solution.py:52
  139.8 2.7 %fusion.47 = f32[16,512,128]{2,1,0:T(8,128)} fusion(f32[16,512,128]{2,1,0:T(8,128)} %get-tuple-element.409, s32[]{:T(128)S(6)} %copy.40, f32[2048,128]{1,0:T(8,128)S(1)} %get-tuple-element.418, s32[2048]{0:T(1024)S(1)} %get-tuple-element.416, s32[512]{0:T(512)S(1)} %iota_add_fusion.7), kind=kOutput, calls=%fused_computation.16.clone.1 | convolution fusion | flops 1611661312 | bytes 1320964 | tf_op jit(solution)/shard_map/while/body/eval_jaxpr/dot_general | solution.py:52
  143.8 2.7 %fusion.47 = f32[16,512,128]{2,1,0:T(8,128)} fusion(f32[16,512,128]{2,1,0:T(8,128)} %get-tuple-element.409, s32[]{:T(128)S(6)} %copy.40, f32[2048,128]{1,0:T(8,128)S(1)} %get-tuple-element.418, s32[2048]{0:T(1024)S(1)} %get-tuple-element.416, s32[512]{0:T(512)S(1)} %iota_add_fusion.7), kind=kOutput, calls=%fused_computation.16.clone.1 | convolution fusion | flops 1611661312 | bytes 1320964 | tf_op jit(solution)/shard_map/while/body/eval_jaxpr/dot_general | solution.py:52
  147.7 2.7 %fusion.47 = f32[16,512,128]{2,1,0:T(8,128)} fusion(f32[16,512,128]{2,1,0:T(8,128)} %get-tuple-element.409, s32[]{:T(128)S(6)} %copy.40, f32[2048,128]{1,0:T(8,128)S(1)} %get-tuple-element.418, s32[2048]{0:T(1024)S(1)} %get-tuple-element.416, s32[512]{0:T(512)S(1)} %iota_add_fusion.7), kind=kOutput, calls=%fused_computation.16.clone.1 | convolution fusion | flops 1611661312 | bytes 1320964 | tf_op jit(solution)/shard_map/while/body/eval_jaxpr/dot_general | solution.py:52
  151.6 2.7 %fusion.47 = f32[16,512,128]{2,1,0:T(8,128)} fusion(f32[16,512,128]{2,1,0:T(8,128)} %get-tuple-element.409, s32[]{:T(128)S(6)} %copy.40, f32[2048,128]{1,0:T(8,128)S(1)} %get-tuple-element.418, s32[2048]{0:T(1024)S(1)} %get-tuple-element.416, s32[512]{0:T(512)S(1)} %iota_add_fusion.7), kind=kOutput, calls=%fused_computation.16.clone.1 | convolution fusion | flops 1611661312 | bytes 1320964 | tf_op jit(solution)/shard_map/while/body/eval_jaxpr/dot_general | solution.py:52
  155.5 2.7 %fusion.47 = f32[16,512,128]{2,1,0:T(8,128)} fusion(f32[16,512,128]{2,1,0:T(8,128)} %get-tuple-element.409, s32[]{:T(128)S(6)} %copy.40, f32[2048,128]{1,0:T(8,128)S(1)} %get-tuple-element.418, s32[2048]{0:T(1024)S(1)} %get-tuple-element.416, s32[512]{0:T(512)S(1)} %iota_add_fusion.7), kind=kOutput, calls=%fused_computation.16.clone.1 | convolution fusion | flops 1611661312 | bytes 1320964 | tf_op jit(solution)/shard_map/while/body/eval_jaxpr/dot_general | solution.py:52
  159.5 2.7 %fusion.47 = f32[16,512,128]{2,1,0:T(8,128)} fusion(f32[16,512,128]{2,1,0:T(8,128)} %get-tuple-element.409, s32[]{:T(128)S(6)} %copy.40, f32[2048,128]{1,0:T(8,128)S(1)} %get-tuple-element.418, s32[2048]{0:T(1024)S(1)} %get-tuple-element.416, s32[512]{0:T(512)S(1)} %iota_add_fusion.7), kind=kOutput, calls=%fused_computation.16.clone.1 | convolution fusion | flops 1611661312 | bytes 1320964 | tf_op jit(solution)/shard_map/while/body/eval_jaxpr/dot_general | solution.py:52
  162.1 3.9 %multiply_reduce_fusion = f32[]{:T(128)} fusion(f32[16,512,128]{2,1,0:T(8,128)} %get-tuple-element.131), kind=kLoop, calls=%fused_computation.27 | loop fusion | flops 2097151 | bytes 4194308 | tf_op jit(solution)/shard_map/reduce_sum | solution.py:104
  166.0 9.8 %psum.28 = f32[]{:T(128)} all-reduce(f32[]{:T(128)} %multiply_reduce_fusion), channel_id=1, replica_groups=mesh['dp_0'=4,'dp_1'=4,'dp_2'=2,'mp'=4] {'dp_0'}, use_global_device_ids=true, to_apply=%region_12.13 | all-reduce | flops 1 | bytes 8 | tf_op jit(solution)/shard_map/psum | solution.py:20
  175.8 9.5 %psum.29 = f32[]{:T(128)} all-reduce(f32[]{:T(128)} %psum.28), channel_id=1, replica_groups=mesh['dp_0'=4,'dp_1'=4,'dp_2'=2,'mp'=4] {'dp_1'}, use_global_device_ids=true, to_apply=%region_13.14 | all-reduce | flops 1 | bytes 8 | tf_op jit(solution)/shard_map/psum | solution.py:20
  185.3 3.1 %psum.30 = f32[]{:T(128)} all-reduce(f32[]{:T(128)} %psum.29), channel_id=1, replica_groups=mesh['dp_0'=4,'dp_1'=4,'dp_2'=2,'mp'=4] {'dp_2'}, use_global_device_ids=true, to_apply=%region_14.15 | all-reduce | flops 1 | bytes 8 | tf_op jit(solution)/shard_map/psum | solution.py:20
  188.4 11.1 %psum.31 = f32[]{:T(128)} all-reduce(f32[]{:T(128)} %psum.30), channel_id=1, replica_groups=mesh['dp_0'=4,'dp_1'=4,'dp_2'=2,'mp'=4] {'mp'}, use_global_device_ids=true, to_apply=%region_15.16 | all-reduce | flops 1 | bytes 8 | tf_op jit(solution)/shard_map/psum | solution.py:20
  200.3 2.7 %broadcast_multiply_fusion = f32[16,512,128]{2,1,0:T(8,128)S(1)} fusion(f32[16,512,128]{2,1,0:T(8,128)} %get-tuple-element.131, f32[]{:T(128)S(6)} %div.34), kind=kLoop, calls=%fused_computation.28 | loop fusion | flops 1048576 | bytes 8388612 | tf_op jit(solution)/shard_map/mul | solution.py:108
  203.0 0.7 copy-done
  203.7 1.3 copy-done.1
  205.0 7.3 %multiply_subtract_fusion = (f32[8192,128]{1,0:T(8,128)}, f32[8192,128]{1,0:T(8,128)}, f32[8192,128]{1,0:T(8,128)}) fusion(f32[8192,128]{1,0:T(8,128)S(1)} %copy-done, f32[16,512,128]{2,1,0:T(8,128)S(1)} %broadcast_multiply_fusion, f32[8192,128]{1,0:T(8,128)S(1)} %copy-done.1, f32[8192,128]{1,0:T(8,128)} %param.15), kind=kLoop, calls=%fused_computation.26 | loop fusion | flops 15728640 | bytes 29360128 | tf_op jit(solution)/shard_map/sub | solution.py:113
  (88 shorter events, 29.1 us)
Async XLA Ops:
  78.7 20.7 %all-to-all-start.1 = ((f32[32,64,128]{2,1,0:T(8,128)}), f32[32,64,128]{2,1,0:T(8,128)S(1)}, u32[]{:S(2)}, u32[]{:S(2)}) async-start(f32[32,64,128]{2,1,0:T(8,128)} %bitcast.7), calls=%async_computation.1 | async-start | bytes 2097152 | tf_op jit(solution)/shard_map/all_to_all | solution.py:97
  200.2 3.5 %copy-start = (f32[8192,128]{1,0:T(8,128)S(1)}, f32[8192,128]{1,0:T(8,128)}, u32[]{:S(2)}) copy-start(f32[8192,128]{1,0:T(8,128)} %param.13) | copy-start | bytes 12582916
  200.2 4.7 %copy-start.1 = (f32[8192,128]{1,0:T(8,128)S(1)}, f32[8192,128]{1,0:T(8,128)}, u32[]{:S(2)}) copy-start(f32[8192,128]{1,0:T(8,128)} %param.14) | copy-start | bytes 12582916
where the time goes:
time: 214 us; the launch traced here: 212 us
  matrix products  53 us (25%)
  blocking collectives  49.1 us (23%)
  other arithmetic  48.4 us (23%)
  local copies, waits for them, and re-layouts  25.9 us (12%)
  waiting for transfers between devices  16.6 us (8%)
  loops' own time  13.8 us (6%)
  starting transfers between devices  3.93 us (2%)
    dot_general x16, matrix products, gather_one_block(): jnp.dot(match.astype(jnp.float32), got, precision=lax.Precision.HIGHEST,...  43 us
    psum x4, blocking collectives, by_axis(): shard = lax.psum(shard, axis)  33.5 us
    all_to_all x1, waiting for transfers between devices, body(): lax.all_to_all(sums.reshape(peers, room, width), DP, split_axis=0, concat...  16.6 us
    all_to_all x1, blocking collectives, body(): lax.all_to_all(row_marks, DP, split_axis=0, concat_axis=0, tiled=True)  15.6 us
    add x16, other arithmetic, gather_one_block(): target = start + jnp.arange(step, dtype=jnp.int32)  10.3 us
    dot_general x4, matrix products, pack_one_block(): jnp.dot(match.astype(jnp.bfloat16), values, preferred_element_type=jnp.fl...  10 us
    dynamic_slice x16, local copies, waits for them, and re-layouts, gather_rows(): lax.map(gather_one_block, block_starts(rows_dev, step))  9.31 us
    reduce_or x4, other arithmetic, first_block(): return jnp.logical_not(jnp.any(earlier, axis=1))  7.6 us
  transfers between devices with their start and end apart: 1, of which 1 were waited for; matrix products, arithmetic and copies ran while one was open for 0% of the time, Pallas kernels for 0%

commit v1 on v0

--- a/solution.py
+++ b/solution.py
@@ -17,7 +17,7 @@
 
 def by_axis(shard, axes):
     for axis in axes:
-        shard = lax.psum(shard, axis)
+        shard = jnp.sum(lax.all_gather(shard, axis), axis=0)
     return shard
 
 

time: 214 us -> 221 us (1.033)
  local copies, waits for them, and re-layouts: 25.9 us -> 34 us
  blocking collectives: 49.1 us -> 46.6 us
  other arithmetic: 48.4 us -> 50.8 us
    psum x4 -> x0, blocking collectives: 33.5 us -> none  [by_axis(): shard = lax.psum(shard, axis)]
    unnamed x0 -> x4, blocking collectives: none -> 30.9 us
    unnamed x5 -> x25, local copies, waits for them, and re-layouts: 1.99 us -> 10.1 us
    reduce_sum x0 -> x4, other arithmetic: none -> 2.41 us  [by_axis(): shard = jnp.sum(lax.all_gather(shard, axis), axis=0)]
where the time goes in v1:
time: 221 us; the launch traced here: 220 us
  matrix products  53 us (24%)
  other arithmetic  50.8 us (23%)
  blocking collectives  46.6 us (21%)
  local copies, waits for them, and re-layouts  34 us (15%)
  waiting for transfers between devices  15.9 us (7%)
  loops' own time  13.8 us (6%)
  starting transfers between devices  3.93 us (2%)
    dot_general x16, matrix products, gather_one_block(): jnp.dot(match.astype(jnp.float32), got, precision=lax.Precision.HIGHEST,...  43 us
    unnamed x4, blocking collectives  30.9 us
    all_to_all x1, waiting for transfers between devices, body(): lax.all_to_all(sums.reshape(peers, room, width), DP, split_axis=0, concat...  15.9 us
    all_to_all x1, blocking collectives, body(): lax.all_to_all(row_marks, DP, split_axis=0, concat_axis=0, tiled=True)  15.6 us
    add x16, other arithmetic, gather_one_block(): target = start + jnp.arange(step, dtype=jnp.int32)  10.3 us
    unnamed x25, local copies, waits for them, and re-layouts  10.1 us
    dot_general x4, matrix products, pack_one_block(): jnp.dot(match.astype(jnp.bfloat16), values, preferred_element_type=jnp.fl...  10 us
    dynamic_slice x16, local copies, waits for them, and re-layouts, gather_rows(): lax.map(gather_one_block, block_starts(rows_dev, step))  9.31 us
  transfers between devices with their start and end apart: 1, of which 1 were waited for; matrix products, arithmetic and copies ran while one was open for 0% of the time, Pallas kernels for 0%

profile of v1, /device:TPU:0, one launch (start us, length us, event | category | flops | bytes accessed | tf_op | source)
XLA Modules:
  0.0 219.6 jit_solution(15470682601935831258)
XLA Ops:
  0.7 0.7 add_select_fusion
  1.4 22.3 %while.46 = (s32[]{:T(128)}, pred[4,512]{1,0:T(4,128)(4,1)S(1)}, s32[2048]{0:T(1024)}, s32[4]{0:T(128)S(1)}, s32[]{:T(128)}, /*index=5*/s32[]{:T(128)}, s32[]{:T(128)}) while((s32[]{:T(128)}, pred[4,512]{1,0:T(4,128)(4,1)S(1)}, s32[2048]{0:T(1024)}, s32[4]{0:T(128)S(1)}, s32[]{:T(128)}, /*index=5*/s32[]{:T(128)}, s32[]{:T(128)}) %tuple.67), condition=%wide.region_2.3_spmd.clone, body=%wide.region_0.2_spmd.clone.sunk | while | flops 4194821 | bytes 22159 | solution.py:79
  4.2 0.8 dynamic_slice.38
  5.0 1.9 fusion.48
  9.8 0.8 dynamic_slice.38
  10.6 1.9 fusion.48
  15.4 0.8 dynamic_slice.38
  16.1 1.9 fusion.48
  20.9 0.8 dynamic_slice.38
  21.7 1.9 fusion.48
  23.7 20.1 %while.43 = (s32[]{:T(128)}, s32[4,512]{1,0:T(4,128)S(1)}, pred[4,512]{1,0:T(4,128)(4,1)S(1)}, s32[2048]{0:T(1024)S(1)}, s32[4]{0:T(128)S(1)}, /*index=5*/s32[2048]{0:T(1024)}, s32[]{:T(128)}, s32[]{:T(128)}, s32[]{:T(128)}) while((s32[]{:T(128)}, s32[4,512]{1,0:T(4,128)S(1)}, pred[4,512]{1,0:T(4,128)(4,1)S(1)}, s32[2048]{0:T(1024)S(1)}, ...), condition=%wide.region_5.6_spmd, body=%wide.region_3.5_spmd.sunk | while | flops 6290949 | bytes 41119 | solution.py:91
  26.1 0.8 dynamic_slice.33
  26.8 1.8 convert_reduce_fusion.3
  31.1 0.8 dynamic_slice.33
  31.9 1.8 convert_reduce_fusion.3
  36.1 0.8 dynamic_slice.33
  36.9 1.8 convert_reduce_fusion.3
  41.1 0.8 dynamic_slice.33
  41.9 1.8 convert_reduce_fusion.3
  43.8 0.7 multiply_subtract_fusion.1
  44.5 18.4 %while.44 = (s32[]{:T(128)}, f32[4,512,128]{2,1,0:T(8,128)}, s32[4,512]{1,0:T(4,128)S(1)}, s32[2048]{0:T(1024)S(1)}, s32[4]{0:T(128)S(1)}, /*index=5*/bf16[2048,...) while((s32[]{:T(128)}, f32[4,512,128]{2,1,0:T(8,128)}, s32[4,512]{1,0:T(4,128)S(1)}, ...), condition=%wide.region_8.9_spmd, body=%wide.region_6.8_spmd.sunk | while | flops 272629760 | bytes 823421 | solution.py:42
  45.2 0.7 iota_add_fusion.6
  45.9 0.7 fusion.44
  46.6 2.5 %fusion.43 = f32[4,512,128]{2,1,0:T(8,128)} fusion(f32[4,512,128]{2,1,0:T(8,128)} %get-tuple-element.385, s32[]{:T(128)S(6)} %copy.32, bf16[2048,128]{1,0:T(8,128)(2,1)} %get-tuple-element.398, s32[2048]{0:T(1024)S(1)} %get-tuple-element.396, s32[512]{0:T(512)S(1)} %iota_add_fusion.6), kind=kOutput, calls=%fused_computation.9.clone.1 | convolution fusion | flops 269484032 | bytes 796676 | tf_op jit(solution)/shard_map/while/body/eval_jaxpr/dot_general | solution.py:38
  49.8 0.7 iota_add_fusion.6
  50.5 0.7 fusion.44
  51.2 2.5 %fusion.43 = f32[4,512,128]{2,1,0:T(8,128)} fusion(f32[4,512,128]{2,1,0:T(8,128)} %get-tuple-element.385, s32[]{:T(128)S(6)} %copy.32, bf16[2048,128]{1,0:T(8,128)(2,1)} %get-tuple-element.398, s32[2048]{0:T(1024)S(1)} %get-tuple-element.396, s32[512]{0:T(512)S(1)} %iota_add_fusion.6), kind=kOutput, calls=%fused_computation.9.clone.1 | convolution fusion | flops 269484032 | bytes 796676 | tf_op jit(solution)/shard_map/while/body/eval_jaxpr/dot_general | solution.py:38
  54.4 0.7 iota_add_fusion.6
  55.8 2.5 %fusion.43 = f32[4,512,128]{2,1,0:T(8,128)} fusion(f32[4,512,128]{2,1,0:T(8,128)} %get-tuple-element.385, s32[]{:T(128)S(6)} %copy.32, bf16[2048,128]{1,0:T(8,128)(2,1)} %get-tuple-element.398, s32[2048]{0:T(1024)S(1)} %get-tuple-element.396, s32[512]{0:T(512)S(1)} %iota_add_fusion.6), kind=kOutput, calls=%fused_computation.9.clone.1 | convolution fusion | flops 269484032 | bytes 796676 | tf_op jit(solution)/shard_map/while/body/eval_jaxpr/dot_general | solution.py:38
  59.0 0.7 iota_add_fusion.6
  60.4 2.5 %fusion.43 = f32[4,512,128]{2,1,0:T(8,128)} fusion(f32[4,512,128]{2,1,0:T(8,128)} %get-tuple-element.385, s32[]{:T(128)S(6)} %copy.32, bf16[2048,128]{1,0:T(8,128)(2,1)} %get-tuple-element.398, s32[2048]{0:T(1024)S(1)} %get-tuple-element.396, s32[512]{0:T(512)S(1)} %iota_add_fusion.6), kind=kOutput, calls=%fused_computation.9.clone.1 | convolution fusion | flops 269484032 | bytes 796676 | tf_op jit(solution)/shard_map/while/body/eval_jaxpr/dot_general | solution.py:38
  63.1 15.6 %all_to_all.11 = f32[32,1,64]{2,1,0:T(1,128)S(1)} all-to-all(f32[32,1,64]{2,1,0:T(1,128)S(1)} %convert_element_type.26), channel_id=1, replica_groups=mesh['dp_0'=4,'dp_1'=4,'dp_2'=2,'mp'=4] {'dp_0','dp_1','dp_2'}, dimensions={0} | all-to-all | bytes 16384 | tf_op jit(solution)/shard_map/all_to_all | solution.py:100
  78.7 3.9 %all-to-all-start.1 = ((f32[32,64,128]{2,1,0:T(8,128)}), f32[32,64,128]{2,1,0:T(8,128)S(1)}, u32[]{:S(2)}, u32[]{:S(2)}) async-start(f32[32,64,128]{2,1,0:T(8,128)} %bitcast.7), calls=%async_computation.1 | async-start | bytes 2097152 | tf_op jit(solution)/shard_map/all_to_all | solution.py:97
  83.5 15.9 %all-to-all-done.1 = f32[32,64,128]{2,1,0:T(8,128)S(1)} async-done(((f32[32,64,128]{2,1,0:T(8,128)}), f32[32,64,128]{2,1,0:T(8,128)S(1)}, u32[]{:S(2)}, u32[]{:S(2)}) %all-to-all-start.1) | async-done | bytes 1048608 | tf_op jit(solution)/shard_map/all_to_all | solution.py:97
  99.4 62.8 %while.45 = (s32[]{:T(128)}, f32[16,512,128]{2,1,0:T(8,128)}, s32[2048]{0:T(1024)S(1)}, s32[16]{0:T(128)S(1)}, f32[2048,128]{1,0:T(8,128)S(1)}, /*index=5*/s32[]{:T(128)}) while((s32[]{:T(128)}, f32[16,512,128]{2,1,0:T(8,128)}, s32[2048]{0:T(1024)S(1)}, s32[16]{0:T(128)S(1)}, f32[2048,128]{1,0:T(8,128)S(1)}, /*index=5*/s32[]{:T(128)}) %tuple.79), condition=%wide.region_10.11_spmd, body=%wide.region_9.10_spmd.sunk | while | flops 1611661824 | bytes 1323105 | solution.py:59
  100.6 2.7 %fusion.47 = f32[16,512,128]{2,1,0:T(8,128)} fusion(f32[16,512,128]{2,1,0:T(8,128)} %get-tuple-element.409, s32[]{:T(128)S(6)} %copy.40, f32[2048,128]{1,0:T(8,128)S(1)} %get-tuple-element.418, s32[2048]{0:T(1024)S(1)} %get-tuple-element.416, s32[512]{0:T(512)S(1)} %iota_add_fusion.7), kind=kOutput, calls=%fused_computation.16.clone.1 | convolution fusion | flops 1611661312 | bytes 1320964 | tf_op jit(solution)/shard_map/while/body/eval_jaxpr/dot_general | solution.py:52
  104.6 2.7 %fusion.47 = f32[16,512,128]{2,1,0:T(8,128)} fusion(f32[16,512,128]{2,1,0:T(8,128)} %get-tuple-element.409, s32[]{:T(128)S(6)} %copy.40, f32[2048,128]{1,0:T(8,128)S(1)} %get-tuple-element.418, s32[2048]{0:T(1024)S(1)} %get-tuple-element.416, s32[512]{0:T(512)S(1)} %iota_add_fusion.7), kind=kOutput, calls=%fused_computation.16.clone.1 | convolution fusion | flops 1611661312 | bytes 1320964 | tf_op jit(solution)/shard_map/while/body/eval_jaxpr/dot_general | solution.py:52
  108.5 2.7 %fusion.47 = f32[16,512,128]{2,1,0:T(8,128)} fusion(f32[16,512,128]{2,1,0:T(8,128)} %get-tuple-element.409, s32[]{:T(128)S(6)} %copy.40, f32[2048,128]{1,0:T(8,128)S(1)} %get-tuple-element.418, s32[2048]{0:T(1024)S(1)} %get-tuple-element.416, s32[512]{0:T(512)S(1)} %iota_add_fusion.7), kind=kOutput, calls=%fused_computation.16.clone.1 | convolution fusion | flops 1611661312 | bytes 1320964 | tf_op jit(solution)/shard_map/while/body/eval_jaxpr/dot_general | solution.py:52
  112.4 2.7 %fusion.47 = f32[16,512,128]{2,1,0:T(8,128)} fusion(f32[16,512,128]{2,1,0:T(8,128)} %get-tuple-element.409, s32[]{:T(128)S(6)} %copy.40, f32[2048,128]{1,0:T(8,128)S(1)} %get-tuple-element.418, s32[2048]{0:T(1024)S(1)} %get-tuple-element.416, s32[512]{0:T(512)S(1)} %iota_add_fusion.7), kind=kOutput, calls=%fused_computation.16.clone.1 | convolution fusion | flops 1611661312 | bytes 1320964 | tf_op jit(solution)/shard_map/while/body/eval_jaxpr/dot_general | solution.py:52
  116.3 2.7 %fusion.47 = f32[16,512,128]{2,1,0:T(8,128)} fusion(f32[16,512,128]{2,1,0:T(8,128)} %get-tuple-element.409, s32[]{:T(128)S(6)} %copy.40, f32[2048,128]{1,0:T(8,128)S(1)} %get-tuple-element.418, s32[2048]{0:T(1024)S(1)} %get-tuple-element.416, s32[512]{0:T(512)S(1)} %iota_add_fusion.7), kind=kOutput, calls=%fused_computation.16.clone.1 | convolution fusion | flops 1611661312 | bytes 1320964 | tf_op jit(solution)/shard_map/while/body/eval_jaxpr/dot_general | solution.py:52
  120.2 2.7 %fusion.47 = f32[16,512,128]{2,1,0:T(8,128)} fusion(f32[16,512,128]{2,1,0:T(8,128)} %get-tuple-element.409, s32[]{:T(128)S(6)} %copy.40, f32[2048,128]{1,0:T(8,128)S(1)} %get-tuple-element.418, s32[2048]{0:T(1024)S(1)} %get-tuple-element.416, s32[512]{0:T(512)S(1)} %iota_add_fusion.7), kind=kOutput, calls=%fused_computation.16.clone.1 | convolution fusion | flops 1611661312 | bytes 1320964 | tf_op jit(solution)/shard_map/while/body/eval_jaxpr/dot_general | solution.py:52
  124.2 2.7 %fusion.47 = f32[16,512,128]{2,1,0:T(8,128)} fusion(f32[16,512,128]{2,1,0:T(8,128)} %get-tuple-element.409, s32[]{:T(128)S(6)} %copy.40, f32[2048,128]{1,0:T(8,128)S(1)} %get-tuple-element.418, s32[2048]{0:T(1024)S(1)} %get-tuple-element.416, s32[512]{0:T(512)S(1)} %iota_add_fusion.7), kind=kOutput, calls=%fused_computation.16.clone.1 | convolution fusion | flops 1611661312 | bytes 1320964 | tf_op jit(solution)/shard_map/while/body/eval_jaxpr/dot_general | solution.py:52
  128.1 2.7 %fusion.47 = f32[16,512,128]{2,1,0:T(8,128)} fusion(f32[16,512,128]{2,1,0:T(8,128)} %get-tuple-element.409, s32[]{:T(128)S(6)} %copy.40, f32[2048,128]{1,0:T(8,128)S(1)} %get-tuple-element.418, s32[2048]{0:T(1024)S(1)} %get-tuple-element.416, s32[512]{0:T(512)S(1)} %iota_add_fusion.7), kind=kOutput, calls=%fused_computation.16.clone.1 | convolution fusion | flops 1611661312 | bytes 1320964 | tf_op jit(solution)/shard_map/while/body/eval_jaxpr/dot_general | solution.py:52
  132.0 2.7 %fusion.47 = f32[16,512,128]{2,1,0:T(8,128)} fusion(f32[16,512,128]{2,1,0:T(8,128)} %get-tuple-element.409, s32[]{:T(128)S(6)} %copy.40, f32[2048,128]{1,0:T(8,128)S(1)} %get-tuple-element.418, s32[2048]{0:T(1024)S(1)} %get-tuple-element.416, s32[512]{0:T(512)S(1)} %iota_add_fusion.7), kind=kOutput, calls=%fused_computation.16.clone.1 | convolution fusion | flops 1611661312 | bytes 1320964 | tf_op jit(solution)/shard_map/while/body/eval_jaxpr/dot_general | solution.py:52
  135.9 2.7 %fusion.47 = f32[16,512,128]{2,1,0:T(8,128)} fusion(f32[16,512,128]{2,1,0:T(8,128)} %get-tuple-element.409, s32[]{:T(128)S(6)} %copy.40, f32[2048,128]{1,0:T(8,128)S(1)} %get-tuple-element.418, s32[2048]{0:T(1024)S(1)} %get-tuple-element.416, s32[512]{0:T(512)S(1)} %iota_add_fusion.7), kind=kOutput, calls=%fused_computation.16.clone.1 | convolution fusion | flops 1611661312 | bytes 1320964 | tf_op jit(solution)/shard_map/while/body/eval_jaxpr/dot_general | solution.py:52
  139.9 2.7 %fusion.47 = f32[16,512,128]{2,1,0:T(8,128)} fusion(f32[16,512,128]{2,1,0:T(8,128)} %get-tuple-element.409, s32[]{:T(128)S(6)} %copy.40, f32[2048,128]{1,0:T(8,128)S(1)} %get-tuple-element.418, s32[2048]{0:T(1024)S(1)} %get-tuple-element.416, s32[512]{0:T(512)S(1)} %iota_add_fusion.7), kind=kOutput, calls=%fused_computation.16.clone.1 | convolution fusion | flops 1611661312 | bytes 1320964 | tf_op jit(solution)/shard_map/while/body/eval_jaxpr/dot_general | solution.py:52
  143.8 2.7 %fusion.47 = f32[16,512,128]{2,1,0:T(8,128)} fusion(f32[16,512,128]{2,1,0:T(8,128)} %get-tuple-element.409, s32[]{:T(128)S(6)} %copy.40, f32[2048,128]{1,0:T(8,128)S(1)} %get-tuple-element.418, s32[2048]{0:T(1024)S(1)} %get-tuple-element.416, s32[512]{0:T(512)S(1)} %iota_add_fusion.7), kind=kOutput, calls=%fused_computation.16.clone.1 | convolution fusion | flops 1611661312 | bytes 1320964 | tf_op jit(solution)/shard_map/while/body/eval_jaxpr/dot_general | solution.py:52
  147.7 2.7 %fusion.47 = f32[16,512,128]{2,1,0:T(8,128)} fusion(f32[16,512,128]{2,1,0:T(8,128)} %get-tuple-element.409, s32[]{:T(128)S(6)} %copy.40, f32[2048,128]{1,0:T(8,128)S(1)} %get-tuple-element.418, s32[2048]{0:T(1024)S(1)} %get-tuple-element.416, s32[512]{0:T(512)S(1)} %iota_add_fusion.7), kind=kOutput, calls=%fused_computation.16.clone.1 | convolution fusion | flops 1611661312 | bytes 1320964 | tf_op jit(solution)/shard_map/while/body/eval_jaxpr/dot_general | solution.py:52
  151.6 2.7 %fusion.47 = f32[16,512,128]{2,1,0:T(8,128)} fusion(f32[16,512,128]{2,1,0:T(8,128)} %get-tuple-element.409, s32[]{:T(128)S(6)} %copy.40, f32[2048,128]{1,0:T(8,128)S(1)} %get-tuple-element.418, s32[2048]{0:T(1024)S(1)} %get-tuple-element.416, s32[512]{0:T(512)S(1)} %iota_add_fusion.7), kind=kOutput, calls=%fused_computation.16.clone.1 | convolution fusion | flops 1611661312 | bytes 1320964 | tf_op jit(solution)/shard_map/while/body/eval_jaxpr/dot_general | solution.py:52
  155.5 2.7 %fusion.47 = f32[16,512,128]{2,1,0:T(8,128)} fusion(f32[16,512,128]{2,1,0:T(8,128)} %get-tuple-element.409, s32[]{:T(128)S(6)} %copy.40, f32[2048,128]{1,0:T(8,128)S(1)} %get-tuple-element.418, s32[2048]{0:T(1024)S(1)} %get-tuple-element.416, s32[512]{0:T(512)S(1)} %iota_add_fusion.7), kind=kOutput, calls=%fused_computation.16.clone.1 | convolution fusion | flops 1611661312 | bytes 1320964 | tf_op jit(solution)/shard_map/while/body/eval_jaxpr/dot_general | solution.py:52
  159.5 2.7 %fusion.47 = f32[16,512,128]{2,1,0:T(8,128)} fusion(f32[16,512,128]{2,1,0:T(8,128)} %get-tuple-element.409, s32[]{:T(128)S(6)} %copy.40, f32[2048,128]{1,0:T(8,128)S(1)} %get-tuple-element.418, s32[2048]{0:T(1024)S(1)} %get-tuple-element.416, s32[512]{0:T(512)S(1)} %iota_add_fusion.7), kind=kOutput, calls=%fused_computation.16.clone.1 | convolution fusion | flops 1611661312 | bytes 1320964 | tf_op jit(solution)/shard_map/while/body/eval_jaxpr/dot_general | solution.py:52
  162.2 3.9 %multiply_reduce_fusion = f32[]{:T(128)} fusion(f32[16,512,128]{2,1,0:T(8,128)} %get-tuple-element.131), kind=kLoop, calls=%fused_computation.27 | loop fusion | flops 2097151 | bytes 4194308 | tf_op jit(solution)/shard_map/reduce_sum | solution.py:104
  166.1 1.4 dynamic-update-slice
  168.1 9.2 %all-reduce = f32[4]{0:T(128)S(1)} all-reduce(f32[4]{0:T(128)S(1)} %dynamic-update-slice), channel_id=1, replica_groups=mesh['dp_0'=4,'dp_1'=4,'dp_2'=2,'mp'=4] {'dp_0'}, use_global_device_ids=true, to_apply=%add | all-reduce | flops 4 | bytes 32
  177.9 1.4 dynamic-update-slice.1
  179.9 8.9 %all-reduce.1 = f32[4]{0:T(128)S(1)} all-reduce(f32[4]{0:T(128)S(1)} %dynamic-update-slice.1), channel_id=1, replica_groups=mesh['dp_0'=4,'dp_1'=4,'dp_2'=2,'mp'=4] {'dp_1'}, use_global_device_ids=true, to_apply=%add.1 | all-reduce | flops 4 | bytes 32
  189.4 1.4 dynamic-update-slice.2
  191.3 2.4 %all-reduce.2 = f32[2]{0:T(128)S(1)} all-reduce(f32[2]{0:T(128)S(1)} %dynamic-update-slice.2), channel_id=1, replica_groups=mesh['dp_0'=4,'dp_1'=4,'dp_2'=2,'mp'=4] {'dp_2'}, use_global_device_ids=true, to_apply=%add.2 | all-reduce | flops 2 | bytes 16
  194.4 1.4 dynamic-update-slice.3
  195.8 10.5 %all-reduce.3 = f32[4]{0:T(128)S(1)} all-reduce(f32[4]{0:T(128)S(1)} %dynamic-update-slice.3), channel_id=1, replica_groups=mesh['dp_0'=4,'dp_1'=4,'dp_2'=2,'mp'=4] {'mp'}, use_global_device_ids=true, to_apply=%add.3 | all-reduce | flops 4 | bytes 32
  207.6 2.7 %broadcast_multiply_fusion = f32[16,512,128]{2,1,0:T(8,128)S(1)} fusion(f32[16,512,128]{2,1,0:T(8,128)} %get-tuple-element.131, f32[]{:T(128)S(6)} %div.34), kind=kLoop, calls=%fused_computation.28 | loop fusion | flops 1048576 | bytes 8388612 | tf_op jit(solution)/shard_map/mul | solution.py:108
  210.3 0.7 copy-done
  211.0 1.3 copy-done.1
  212.3 7.3 %multiply_subtract_fusion = (f32[8192,128]{1,0:T(8,128)}, f32[8192,128]{1,0:T(8,128)}, f32[8192,128]{1,0:T(8,128)}) fusion(f32[8192,128]{1,0:T(8,128)S(1)} %copy-done, f32[16,512,128]{2,1,0:T(8,128)S(1)} %broadcast_multiply_fusion, f32[8192,128]{1,0:T(8,128)S(1)} %copy-done.1, f32[8192,128]{1,0:T(8,128)} %param.15), kind=kLoop, calls=%fused_computation.26 | loop fusion | flops 15728640 | bytes 29360128 | tf_op jit(solution)/shard_map/sub | solution.py:113
  (112 shorter events, 36.7 us)
Async XLA Ops:
  44.5 38.1 %copy-start.5 = (u32[128]{0:T(128)S(1)}, u32[128]{0:T(128)}, u32[]{:S(2)}) copy-start(u32[128]{0:T(128)} %constant.94) | copy-start | bytes 1540
  78.7 20.7 %all-to-all-start.1 = ((f32[32,64,128]{2,1,0:T(8,128)}), f32[32,64,128]{2,1,0:T(8,128)S(1)}, u32[]{:S(2)}, u32[]{:S(2)}) async-start(f32[32,64,128]{2,1,0:T(8,128)} %bitcast.7), calls=%async_computation.1 | async-start | bytes 2097152 | tf_op jit(solution)/shard_map/all_to_all | solution.py:97
  162.2 5.4 %copy-start.4 = (u32[128]{0:T(128)S(1)}, u32[128]{0:T(128)}, u32[]{:S(2)}) copy-start(u32[128]{0:T(128)} %constant.99) | copy-start | bytes 1540
  162.2 17.1 %copy-start.3 = (u32[128]{0:T(128)S(1)}, u32[128]{0:T(128)}, u32[]{:S(2)}) copy-start(u32[128]{0:T(128)} %constant.104) | copy-start | bytes 1540
  162.2 28.6 %copy-start.2 = (u32[128]{0:T(128)S(1)}, u32[128]{0:T(128)}, u32[]{:S(2)}) copy-start(u32[128]{0:T(128)} %constant.109) | copy-start | bytes 1540
  207.6 3.5 %copy-start = (f32[8192,128]{1,0:T(8,128)S(1)}, f32[8192,128]{1,0:T(8,128)}, u32[]{:S(2)}) copy-start(f32[8192,128]{1,0:T(8,128)} %param.13) | copy-start | bytes 12582916
  207.6 4.7 %copy-start.1 = (f32[8192,128]{1,0:T(8,128)S(1)}, f32[8192,128]{1,0:T(8,128)}, u32[]{:S(2)}) copy-start(f32[8192,128]{1,0:T(8,128)} %param.14) | copy-start | bytes 12582916
